TPU v7x, 32 devices: a whole 2x2x4 slice. The times are simulated.
32 devices in a mesh: kpt: 2 (over x), gx: 16 (over z, y, core).
Axes of the slice: x: 2, y: 2, z: 4, core: 2. Of those that a mesh axis runs over, the one named last changes fastest.
Arguments:
- e_field: float32 [2, 3, 64, 512, 128], P(None, None, ('kpt', 'gx')), parts along dimension 2, may hold values from -6 to 6
- h_field: float32 [2, 3, 64, 512, 128], P(None, None, ('kpt', 'gx')), parts along dimension 2, may hold values from -6 to 6
- labels: int32 [64, 512, 128], P(('kpt', 'gx')), parts along dimension 0, may hold values from 0 to 3
- kpoint: int32 [4], P('kpt'), parts along dimension 0, may hold values from 0 to 15
- eps_inf: float32 [4], replicated, may hold values from 1 to 12
- delta_eps: float32 [4], replicated, may hold values from 0.5 to 4
- omega_zero: float32 [4], replicated, may hold values from 0.2 to 1
- damping: float32 [4], replicated, may hold values from 0.05 to 0.8
Outputs:
- e_final: float32 [2, 3, 64, 512, 128], P(None, None, ('kpt', 'gx')), parts along dimension 2
- h_final: float32 [2, 3, 64, 512, 128], P(None, None, ('kpt', 'gx')), parts along dimension 2
There are 2 independent parts, one for each index of `kpt`. A program takes and returns all parts, laid end to end along the dimension named above; an argument that names none is the same for every part. Nothing has to cross between parts.
Inputs may be any that keep to these rules, and one draw needn't show every extreme that they name: `kpoint`: entry 0 indexes the k-point along x, entry 1 along y, out of 16 each.
All inputs are finite; a program needn't handle non-finite values.
Results may differ from a plain program's by a relative error of at most 0.00002.
Values sent between devices are 32-bit elements; how exact they have to be, the bound alone decides.
A program may use at most 128 MiB of HBM per device.

v0:
```python
import functools
import math

import jax
import jax.numpy as jnp
from jax import lax
from jax.experimental import pallas as pl
from jax.experimental.pallas import tpu as pltpu
from jax.sharding import PartitionSpec as P

ITERS = 12
KGRID = 16
CHUNKS = 4
BLOCK = 8
UNROLL = 2
PAD = 8

time_step = 0.5


class Tile:
    def __init__(self, refs, sems, left, right, turns):
        self.e, self.h, self.pol, self.cur, self.coef, self.lab, self.ge, self.gh = refs[:8]
        self.e_stage, self.h_stage, self.e_edge, self.h_edge = refs[8:]
        self.se, self.re, self.sh, self.rh = sems
        self.left, self.right = left, right
        self.turn_r, self.turn_l, self.turn_up, self.turn_down = turns
        self.planes, self.rows, self.width = self.lab.shape
        self.chunk = self.rows // CHUNKS

    def send_e(self, c):
        here = pl.ds(c * self.chunk, self.chunk)
        return pltpu.make_async_remote_copy(
            src_ref=self.e.at[:, pl.ds(1, 2), 0, here], dst_ref=self.ge.at[:, :, here],
            send_sem=self.se.at[c], recv_sem=self.re.at[c],
            device_id={"gx": self.left}, device_id_type=pl.DeviceIdType.MESH)

    def send_h(self, c):
        here, there = pl.ds(c * self.chunk, self.chunk), pl.ds(c * self.chunk + PAD, self.chunk)
        return pltpu.make_async_remote_copy(
            src_ref=self.h.at[:, pl.ds(1, 2), self.planes - 1, there], dst_ref=self.gh.at[:, :, here],
            send_sem=self.sh.at[c], recv_sem=self.rh.at[c],
            device_id={"gx": self.right}, device_id_type=pl.DeviceIdType.MESH)

    def clear(self, table):
        zero = jnp.zeros((BLOCK, self.width), jnp.float32)

        @pl.loop(0, self.rows // BLOCK)
        def _(i):
            here = pl.ds(pl.multiple_of(i * BLOCK, BLOCK), BLOCK)
            for x in range(self.planes):
                label = self.lab[x, here]
                masks = [label == k for k in range(table.shape[1])]
                for which in range(4):
                    picked = zero
                    for k, mask in enumerate(masks):
                        picked = picked + jnp.where(mask, table[which, k], jnp.float32(0.0))
                    self.coef[which, x, here] = picked
                for ri in range(2):
                    for a in range(3):
                        self.pol[ri, a, x, here] = zero
                        self.cur[ri, a, x, here] = zero

    def stage_e(self):
        for x in range(self.planes):
            for ri in range(2):
                for j, a in enumerate((0, 2)):
                    row = 2 * ri + j
                    self.e_stage[x, row:row + 1] = self.e[ri, a, x, 0:1]

    def stage_h(self):
        end = PAD + self.rows - 1
        for x in range(self.planes):
            for ri in range(2):
                for j, a in enumerate((0, 2)):
                    row = 2 * ri + j
                    self.h_stage[x, row:row + 1] = self.h[ri, a, x, end:end + 1]

    def take_edge(self, edge, field, at, turn):
        for x in range(self.planes):
            for j, a in enumerate((0, 2)):
                re, im = turned(edge[x, j:j + 1], edge[x, 2 + j:3 + j], *turn)
                field[0, a, x, at:at + 1] = re
                field[1, a, x, at:at + 1] = im

    def take_e(self):
        self.take_edge(self.e_edge, self.e, self.rows, self.turn_up)

    def take_h(self):
        self.take_edge(self.h_edge, self.h, PAD - 1, self.turn_down)

    def magnetic(self, x, r, next_z, prev_z):
        e, h, ge = self.e, self.h, self.ge
        here = pl.ds(pl.multiple_of(r, BLOCK), BLOCK)
        there = pl.ds(pl.multiple_of(r + PAD, 8), BLOCK)
        up = pl.ds(r + 1, BLOCK)
        if x == self.planes - 1:
            beyond = [turned(ge[0, a, here], ge[1, a, here], *self.turn_r) for a in range(2)]
        else:
            beyond = [(e[0, a, x + 1, here], e[1, a, x + 1, here]) for a in (1, 2)]
        for ri in range(2):
            ex, ey, ez = [e[ri, a, x, here] for a in range(3)]
            cx = (e[ri, 2, x, up] - ez) - (next_z(ey) - ey)
            cy = (next_z(ex) - ex) - (beyond[1][ri] - ez)
            cz = (beyond[0][ri] - ey) - (e[ri, 0, x, up] - ex)
            for a, curl in enumerate((cx, cy, cz)):
                h[ri, a, x, there] = h[ri, a, x, there] - time_step * curl

    def electric(self, x, r, next_z, prev_z):
        e, h, gh, pol, cur = self.e, self.h, self.gh, self.pol, self.cur
        here = pl.ds(pl.multiple_of(r, BLOCK), BLOCK)
        there = pl.ds(pl.multiple_of(r + PAD, 8), BLOCK)
        down = pl.ds(r + PAD - 1, BLOCK)
        ce, ja, jb, de = [self.coef[k, x, here] for k in range(4)]
        if x == 0:
            before = [turned(gh[0, a, here], gh[1, a, here], *self.turn_l) for a in range(2)]
        else:
            before = [(h[0, a, x - 1, there], h[1, a, x - 1, there]) for a in (1, 2)]
        for ri in range(2):
            hx, hy, hz = [h[ri, a, x, there] for a in range(3)]
            kx = (hz - h[ri, 2, x, down]) - (hy - prev_z(hy))
            ky = (hx - prev_z(hx)) - (hz - before[1][ri])
            kz = (hy - before[0][ri]) - (hx - h[ri, 0, x, down])
            for a, kurl in enumerate((kx, ky, kz)):
                field, polar = e[ri, a, x, here], pol[ri, a, x, here]
                current = ja * cur[ri, a, x, here] + jb * (de * field - polar)
                cur[ri, a, x, here] = current
                pol[ri, a, x, here] = polar + time_step * current
                e[ri, a, x, here] = field + ce * (kurl - current)

    def sweep(self, update, order, c, shifts):
        def one(i, carry):
            for x in order:
                update(x, c * self.chunk + i * BLOCK, *shifts)
            return carry
        lax.fori_loop(0, self.chunk // BLOCK, one, 0, unroll=UNROLL)


def turned(re, im, cosv, sinv):
    return re * cosv - im * sinv, re * sinv + im * cosv


def kernel(e_in, h_in, lab_in, table, phase, e_out, h_out, *scratch):
    gx = lax.axis_size("gx")
    me = lax.axis_index("gx")
    q = lax.rem(me, 4)
    base = me - q
    y = lax.div(q, 2)
    core = lax.rem(q, 2)
    local = lab_in.shape[0]
    own_refs, moved_refs = scratch[:12], scratch[12:24]
    own_sems, moved_sems = scratch[24:28], scratch[28:32]
    in_sem, out_sem, sl, rl, so, ro, ees, eer, hhs, hhr = scratch[32:]
    ph = [phase[i] for i in range(12)]
    one, nought = jnp.float32(1.0), jnp.float32(0.0)
    cos_y, sin_y = ph[8], ph[9]
    own = Tile(own_refs, own_sems, lax.rem(me + gx - 1, gx), lax.rem(me + 1, gx),
               ((ph[0], ph[1]), (ph[2], ph[3]), (one, nought), (cos_y, -sin_y)))
    moved = Tile(moved_refs, moved_sems,
                 lax.rem(me + gx - 3 + 2 * core, gx), lax.rem(me + 3 - 2 * (1 - core), gx),
                 ((ph[4], ph[5]), (ph[6], ph[7]), (ph[10], ph[11]), (one, nought)))
    tiles = (own, moved)
    keep, part, width = own.rows, moved.rows, own.width

    def remote(src, dst, send, recv, to):
        return pltpu.make_async_remote_copy(
            src_ref=src, dst_ref=dst, send_sem=send, recv_sem=recv,
            device_id={"gx": to}, device_id_type=pl.DeviceIdType.MESH)

    loads = [
        pltpu.make_async_copy(lab_in.at[:, pl.ds(0, keep)], own.lab, in_sem.at[0]),
        pltpu.make_async_copy(e_in.at[:, :, :, pl.ds(0, keep)], own.e.at[:, :, :, pl.ds(0, keep)], in_sem.at[1]),
        pltpu.make_async_copy(h_in.at[:, :, :, pl.ds(0, keep)], own.h.at[:, :, :, pl.ds(PAD, keep)], in_sem.at[2]),
    ]
    for load in loads:
        load.start()

    barrier = pltpu.get_barrier_semaphore()
    others = [base + lax.rem(q + k, 4) for k in (1, 2, 3)]
    others += [lax.rem(me + gx + k, gx) for k in (-3, -1, 1, 3)]
    for other in others:
        pl.semaphore_signal(barrier, inc=1, device_id={"gx": other},
                            device_id_type=pl.DeviceIdType.MESH)
    pl.semaphore_wait(barrier, len(others))

    def move_in(half, slot):
        rows = pl.ds(keep + half * part, part)
        planes = pl.ds(slot * local, local)
        return ((e_in.at[:, :, :, rows], moved.e.at[:, :, planes, pl.ds(0, part)]),
                (lab_in.at[:, rows], moved.lab.at[planes]),
                (h_in.at[:, :, :, rows], moved.h.at[:, :, planes, pl.ds(PAD, part)]))

    def each_move_in(act):
        for half in range(2):
            self_q = 3 * half
            for k, (src, dst) in enumerate(move_in(half, self_q % 2)):
                @pl.when(q == self_q)
                def _():
                    act(None, pltpu.make_async_copy(src, dst, rl.at[k, self_q % 2]))
            for slot in range(2):
                for k, (src, dst) in enumerate(move_in(half, slot)):
                    @pl.when((q != self_q) & (core == slot))
                    def _():
                        act(remote(src, dst, sl.at[k, half], rl.at[k, slot], base + 2 * half + y), None)

    each_move_in(lambda far, near: (far or near).start())

    def wait_in(k):
        for slot in range(2):
            src, dst = move_in(0, slot)[k]
            remote(src, dst, sl.at[k, 0], rl.at[k, slot], base + lax.rem(q + 1, 4)).wait_recv()

    def edges(f, o_stage, a_stage, o_edge, a_edge, ss, rs, act):
        for slot in range(2):
            src, dst = o_stage, a_edge.at[pl.ds(slot * local, local)]

            @pl.when((core == slot) & (q != 3 * f))
            def _():
                act(remote(src, dst, ss.at[0], rs.at[1 + slot], base + 2 * f + y), None)
        @pl.when(q == 3 * f)
        def _():
            act(None, pltpu.make_async_copy(o_stage, a_edge.at[pl.ds(f * local, local)], rs.at[1 + f]))
        for i in range(2):
            src, dst = a_stage.at[pl.ds(i * local, local)], o_edge
            if i == 1 - f:
                here = (y == 1 - f) & (core == 1 - f)
                away = (y == 1 - f) & (core != 1 - f)

                @pl.when(here)
                def _():
                    act(None, pltpu.make_async_copy(src, dst, rs.at[0]))
            else:
                away = y == 1 - f

            @pl.when(away)
            def _():
                act(remote(src, dst, ss.at[1 + i], rs.at[0], base + 2 * core + i), None)

        @pl.when(y == f)
        def _():
            act(remote(a_stage, a_edge, ss.at[3], rs.at[1], base + 2 * (1 - f) + core), None)

    def edges_arrive(f, o_stage, a_stage, o_edge, a_edge, ss, rs):
        to = base + lax.rem(q + 1, 4)
        remote(o_stage, o_edge, ss.at[0], rs.at[0], to).wait_recv()

        @pl.when(y == f)
        def _():
            for slot in range(2):
                remote(o_stage, a_edge.at[pl.ds(slot * local, local)], ss.at[0], rs.at[1 + slot], to).wait_recv()

        @pl.when(y != f)
        def _():
            remote(a_stage, a_edge, ss.at[3], rs.at[1], to).wait_recv()

    e_edges = (1, own.e_stage, moved.e_stage, own.e_edge, moved.e_edge, ees, eer)
    h_edges = (0, own.h_stage, moved.h_stage, own.h_edge, moved.h_edge, hhs, hhr)

    def start(far, near):
        (far or near).start()

    def sent(far, near):
        if far is not None:
            far.wait_send()

    lane = lax.broadcasted_iota(jnp.int32, (BLOCK, width), 1)
    not_end = lane < width - 1
    not_start = lane > 0

    def next_z(f):
        return jnp.where(not_end, pltpu.roll(f, width - 1, 1), 0.0)

    def prev_z(f):
        return jnp.where(not_start, pltpu.roll(f, 1, 1), 0.0)

    shifts = (next_z, prev_z)
    sequence = [c ^ 1 for c in range(CHUNKS)]

    loads[0].wait()
    own.clear(table)
    loads[1].wait()
    for c in sequence:
        own.send_e(c).start()
    wait_in(0)
    for c in sequence:
        moved.send_e(c).start()
    own.stage_e()
    moved.stage_e()
    wait_in(1)
    moved.clear(table)
    edges(*e_edges, start)
    loads[2].wait()
    wait_in(2)

    def store(k, ref, out):
        rows = pl.ds(0, keep)
        skip = pl.ds(PAD if k else 0, keep)
        return pltpu.make_async_copy(ref.at[:, :, :, skip], out.at[:, :, :, rows], out_sem.at[k])

    def each_move_out(k, ref, out, act):
        for half in range(2):
            rows = pl.ds(keep + half * part, part)
            for i in range(2):
                src = ref.at[:, :, pl.ds(i * local, local), pl.ds(PAD if k else 0, part)]
                dst = out.at[:, :, :, rows]
                away = y == half
                if i == half:
                    @pl.when((y == half) & (core == half))
                    def _():
                        act(None, pltpu.make_async_copy(src, dst, ro.at[k, half]))
                    away = away & (core != half)

                @pl.when(away)
                def _():
                    act(remote(src, dst, so.at[k, i], ro.at[k, half], base + 2 * core + i), None)

    def wait_out(k, ref, out):
        for half in range(2):
            src = ref.at[:, :, pl.ds(0, local), pl.ds(PAD if k else 0, part)]
            dst = out.at[:, :, :, pl.ds(keep + half * part, part)]
            remote(src, dst, so.at[k, 0], ro.at[k, half], base + lax.rem(q + 1, 4)).wait_recv()

    @pl.loop(0, ITERS)
    def _(step):
        for c in sequence:
            if c == CHUNKS - 1:
                edges_arrive(*e_edges)
                for tile in tiles:
                    tile.take_e()
            for tile in tiles:
                @pl.when(step > 0)
                def _():
                    tile.send_h(c).wait_send()
                tile.send_e(c).wait_recv()
                tile.sweep(tile.magnetic, range(tile.planes - 1, -1, -1), c, shifts)
                tile.send_h(c).start()
            if c == CHUNKS - 1:
                @pl.when(step > 0)
                def _():
                    edges(*h_edges, sent)
                for tile in tiles:
                    tile.stage_h()
                edges(*h_edges, start)

        @pl.when(step == ITERS - 1)
        def _():
            store(1, own.h, h_out).start()
            each_move_out(1, moved.h, h_out, start)

        for c in sequence:
            if c == 0:
                edges_arrive(*h_edges)
                for tile in tiles:
                    tile.take_h()
            for tile in tiles:
                tile.send_e(c).wait_send()
                tile.send_h(c).wait_recv()
                tile.sweep(tile.electric, range(tile.planes), c, shifts)

                @pl.when(step < ITERS - 1)
                def _():
                    tile.send_e(c).start()
            if c == 0:
                edges(*e_edges, sent)

                @pl.when(step < ITERS - 1)
                def _():
                    for tile in tiles:
                        tile.stage_e()
                    edges(*e_edges, start)

    store(0, own.e, e_out).start()
    each_move_out(0, moved.e, e_out, start)
    each_move_in(sent)
    edges(*h_edges, sent)
    for c in range(CHUNKS):
        for tile in tiles:
            tile.send_h(c).wait_send()
    for k, ref, mref, out in ((0, own.e, moved.e, e_out), (1, own.h, moved.h, h_out)):
        store(k, ref, out).wait()
        each_move_out(k, mref, out, sent)
        wait_out(k, mref, out)


def shards(e_field, h_field, labels, kpoint, eps_inf, delta_eps, omega_zero, damping):
    theta_x = jnp.float32(2.0 * math.pi) * kpoint[0].astype(jnp.float32) / KGRID
    theta_y = jnp.float32(2.0 * math.pi) * kpoint[1].astype(jnp.float32) / KGRID
    cos_x, sin_x = (jnp.cos(theta_x), jnp.sin(theta_x))
    cos_y, sin_y = (jnp.cos(theta_y), jnp.sin(theta_y))
    half = damping * time_step / 2.0
    table = jnp.stack([
        time_step / eps_inf,
        (1.0 - half) / (1.0 + half),
        time_step * omega_zero * omega_zero / (1.0 + half),
        delta_eps,
    ])
    position = lax.axis_index("gx")
    at_first = position == 0
    at_last = position == lax.axis_size("gx") - 1
    one, nought = jnp.float32(1.0), jnp.float32(0.0)
    size = lax.axis_size("gx")
    y = lax.rem(lax.div(position, 2), 2)
    moved_first = (position < 4) & (lax.rem(position, 2) == 0)
    moved_last = (position >= size - 4) & (lax.rem(position, 2) == 1)

    def turn(where, cosv, sinv):
        return [jnp.where(where, cosv, one), jnp.where(where, sinv, nought)]

    phase = jnp.stack(
        turn(at_last, cos_x, sin_x) + turn(at_first, cos_x, -sin_x)
        + turn(moved_last, cos_x, sin_x) + turn(moved_first, cos_x, -sin_x)
        + [cos_y, sin_y] + turn(y == 1, cos_y, sin_y))
    planes, rows, width = labels.shape
    state = (2, 3, planes, rows, width)

    def tile_scratch(planes, rows):
        field = (2, 3, planes, rows, width)
        padded = (2, 3, planes, rows + PAD, width)
        return ([pltpu.VMEM(shape, jnp.float32) for shape in (padded, padded, field, field, (4, planes, rows, width))]
                + [pltpu.VMEM((planes, rows, width), jnp.int32)]
                + [pltpu.VMEM((2, 2, rows, width), jnp.float32)] * 2
                + [pltpu.VMEM((planes, 8, width), jnp.float32)] * 4)

    dma = pltpu.SemaphoreType.DMA
    anywhere = pl.BlockSpec(memory_space=pl.ANY)
    scalars = pl.BlockSpec(memory_space=pltpu.SMEM)
    return pl.pallas_call(
        kernel,
        out_shape=(jax.ShapeDtypeStruct(state, jnp.float32),) * 2,
        in_specs=[anywhere] * 3 + [scalars] * 2,
        out_specs=(anywhere, anywhere),
        scratch_shapes=tile_scratch(planes, rows // 2) + tile_scratch(2 * planes, rows // 4)
        + [dma((CHUNKS,))] * 8
        + [dma((3,)), dma((2,)), dma((3, 2)), dma((3, 2)), dma((2, 2)), dma((2, 2))]
        + [dma((4,)), dma((3,)), dma((4,)), dma((3,))],
        compiler_params=pltpu.CompilerParams(collective_id=0, has_side_effects=True),
    )(e_field, h_field, labels, table, phase)


def solution(mesh):
    placed = (
        P(None, None, ("kpt", "gx"), None, None),
        P(None, None, ("kpt", "gx"), None, None),
        P(("kpt", "gx"), None, None),
        P("kpt"),
        P(),
        P(),
        P(),
        P(),
    )
    return jax.shard_map(
        shards,
        mesh=mesh,
        in_specs=placed,
        out_specs=(
            P(None, None, ("kpt", "gx"), None, None),
            P(None, None, ("kpt", "gx"), None, None),
        ),
        check_vma=False,
    )
```

profile of v0, /device:TPU:1, one launch (start us, length us, event | category | flops | bytes accessed | tf_op | source)
XLA Modules:
  0.0 243.6 jit_solution(15199335872050703310)
XLA Ops:
  0.7 1.3 fusion.3
  3.6 0.6 stack.65.phase
  4.2 0.7 fusion.1
  4.9 1.2 pad_maximum_fusion.table
  6.2 231.9 %shard_map.95 = (f32[2,3,2,512,128]{4,3,2,1,0:T(8,128)}, f32[2,3,2,512,128]{4,3,2,1,0:T(8,128)}) custom-call(f32[2,3,2,512,128]{4,3,2,1,0:T(8,128)} %e_in.1, f32[2,3,2,512,128]{4,3,2,1,0:T(8,128)} %h_in.1, s32[2,512,128]{2,1,0:T(8,128)} %lab_in.1, f32[4,4]{1,0:T(4,128)} %pad_maximum_fusion.table, f32[12]{0:T(128)} %stack.65.phase), custom_call_target="tpu_custom_call" | custom-call | tf_op jit(solution)/shard_map/pallas_call | solution.py:427
  238.0 0.0 copy-start
  238.1 3.9 %copy.12 = f32[2,3,2,512,128]{4,3,2,1,0:T(8,128)} copy(f32[2,3,2,512,128]{4,3,2,1,0:T(8,128)} %get-tuple-element.9) | data formatting | bytes 6291456
  242.0 0.0 copy-done
  242.0 1.7 copy.13
Async XLA Ops:
  238.0 3.9 %copy-start = (f32[2,3,2,512,128]{4,3,2,1,0:T(8,128)S(1)}, f32[2,3,2,512,128]{4,3,2,1,0:T(8,128)}, u32[]{:S(2)}) copy-start(f32[2,3,2,512,128]{4,3,2,1,0:T(8,128)} %get-tuple-element.10) | copy-start | bytes 9437188
where the time goes:
time: 244 us
  Pallas kernels  232 us (95%)
  local copies, waits for them, and re-layouts  7.49 us (3%)
    pallas_call x1, Pallas kernels, shards(): pl.pallas_call(kernel, out_shape=(jax.ShapeDtypeStruct(state, jnp.float32...  232 us
    unnamed x4, local copies, waits for them, and re-layouts  5.57 us

commit v1 on v0

v1 whole, which is shorter than its diff:
```python
import math

import jax
import jax.numpy as jnp
from jax import lax
from jax.experimental import pallas as pl
from jax.experimental.pallas import tpu as pltpu
from jax.sharding import PartitionSpec as P

ITERS = 12
KGRID = 16
BLOCK = 8
CHUNKS = 7
LAG = 2
UNROLL = 5
LOW = 24
GHOST = 16
BASE = 13

time_step = 0.5


def turned(re, im, cosv, sinv):
    return re * cosv - im * sinv, re * sinv + im * cosv


def chunk_sizes(half):
    blocks = (half + 24) // BLOCK
    return [BLOCK * (blocks // CHUNKS + (c < blocks % CHUNKS)) for c in range(CHUNKS)]


def edges_of(half):
    starts = [0]
    for size in chunk_sizes(half):
        starts.append(starts[-1] + size)
    return starts


def pieces_in(half):
    starts = edges_of(half)
    pieces = []
    for c in range(CHUNKS):
        lo = starts[c] + 16 if c else LOW - GHOST
        hi = starts[c + 1] + 16
        cuts = [lo] + [k for k in (LOW, LOW + half) if lo < k < hi] + [hi]
        pieces.append(list(zip(cuts[:-1], cuts[1:])))
    return pieces


def pieces_out(half):
    starts = edges_of(half)
    return [(max(starts[c], LOW), min(starts[c + 1], LOW + half)) for c in range(CHUNKS)]


def kernel(e_in, h_in, lab_in, table, phase, e_out, h_out,
           e, h, pol, cur, coef, lab, *scratch):
    stages = [scratch[4 * c:4 * c + 4] for c in range(CHUNKS)]
    in_send, in_recv, se, re, sh, rh, so, ro = scratch[4 * CHUNKS:]
    gx = lax.axis_size("gx")
    me = lax.axis_index("gx")
    q = lax.rem(me, 4)
    base = me - q
    y = lax.div(q, 2)
    core = lax.rem(q, 2)
    left = lax.rem(me + gx - 3 + 2 * core, gx)
    right = lax.rem(me + 1 + 2 * core, gx)
    local, total_rows, width = lab_in.shape
    half = total_rows // 2
    planes = 2 * local
    rows = lab.shape[1]
    starts = edges_of(half)
    sizes = chunk_sizes(half)
    ins, outs = pieces_in(half), pieces_out(half)
    ph = [phase[i] for i in range(8)]
    turn_r, turn_l, turn_low, turn_high = [(ph[2 * i], ph[2 * i + 1]) for i in range(4)]

    def remote(src, dst, send, recv, to):
        return pltpu.make_async_remote_copy(
            src_ref=src, dst_ref=dst, send_sem=send, recv_sem=recv,
            device_id={"gx": to}, device_id_type=pl.DeviceIdType.MESH)

    barrier = pltpu.get_barrier_semaphore()
    others = [base + lax.rem(q + k, 4) for k in (1, 2, 3)]
    others += [lax.rem(me + gx + k, gx) for k in (-3, -1, 1, 3)]
    for other in others:
        pl.semaphore_signal(barrier, inc=1, device_id={"gx": other},
                            device_id_type=pl.DeviceIdType.MESH)
    pl.semaphore_wait(barrier, len(others))

    segments = [(c, seg) for c in range(CHUNKS) for seg in ins[c]]

    def move_in(n, dest, slot):
        lo, hi = segments[n][1]
        first = (dest * half + lo - LOW) % total_rows
        src, dst = pl.ds(first, hi - lo), pl.ds(lo, hi - lo)
        group = pl.ds(slot * local, local)
        return ((lab_in.at[:, src], lab.at[group, dst]),
                (e_in.at[:, :, :, src], e.at[:, :, group, dst]),
                (h_in.at[:, :, :, src], h.at[:, :, group, dst]))

    def each_move_in(n, act):
        for dest in range(2):
            for slot in range(2):
                for k, (src, dst) in enumerate(move_in(n, dest, slot)):
                    away = core == slot
                    if dest == slot:
                        @pl.when((y == dest) & (core == slot))
                        def _():
                            act(None, pltpu.make_async_copy(src, dst, in_recv.at[n, k, slot]))
                        away = away & (y != dest)

                    @pl.when(away)
                    def _():
                        act(remote(src, dst, in_send.at[n, k, dest], in_recv.at[n, k, slot], base + 2 * dest + y), None)

    def start(far, near):
        (far or near).start()

    def sent(far, near):
        if far is not None:
            far.wait_send()

    for n in range(len(segments)):
        each_move_in(n, start)

    def wait_in(n, k):
        for slot in range(2):
            src, dst = move_in(n, 0, slot)[k]
            remote(src, dst, in_send.at[n, k, 0], in_recv.at[n, k, slot], base + lax.rem(q + 1, 4)).wait_recv()

    def move_out(c, k, i):
        lo, hi = outs[c]
        ref, out = ((e, e_out), (h, h_out))[k]
        src = ref.at[:, :, pl.ds(i * local, local), pl.ds(lo, hi - lo)]
        to = pl.multiple_of(y * half + (lo - LOW), BLOCK)
        return src, out.at[:, :, :, pl.ds(to, hi - lo)]

    def each_move_out(c, act):
        for k in range(2):
            for i in range(2):
                src, dst = move_out(c, k, i)
                here = (core == i) & (y == i)

                @pl.when(here)
                def _():
                    act(None, pltpu.make_async_copy(src, dst, ro.at[c, k, i]))

                @pl.when(jnp.logical_not(here))
                def _():
                    act(remote(src, dst, so.at[c, k, i], ro.at[c, k, y], base + 2 * core + i), None)

    def wait_out(c):
        for k in range(2):
            for other in range(2):
                src, dst = move_out(c, k, 0)
                remote(src, dst, so.at[c, k, 0], ro.at[c, k, other], base + lax.rem(q + 1, 4)).wait_recv()

    def send_e(c, par):
        return remote(stages[c][0], stages[c][2].at[par], se.at[c], re.at[c, par], left)

    def send_h(c, par):
        return remote(stages[c][1], stages[c][3].at[par], sh.at[c], rh.at[c, par], right)

    lane = lax.broadcasted_iota(jnp.int32, (BLOCK, width), 1)
    not_end = lane < width - 1
    not_start = lane > 0
    zero = jnp.zeros((BLOCK, width), jnp.float32)

    def next_z(f):
        return jnp.where(not_end, pltpu.roll(f, width - 1, 1), 0.0)

    def prev_z(f):
        return jnp.where(not_start, pltpu.roll(f, 1, 1), 0.0)

    @pl.loop(0, rows // BLOCK)
    def _(i):
        here = pl.ds(pl.multiple_of(i * BLOCK, BLOCK), BLOCK)
        for x in range(planes):
            for ri in range(2):
                for a in range(3):
                    pol[ri, a, x, here] = zero
                    cur[ri, a, x, here] = zero

    for x in range(planes):
        for which in range(4):
            coef[which, x, 0:BLOCK] = zero
        for ri in range(2):
            for a in range(3):
                e[ri, a, x, 0:BLOCK] = zero
                h[ri, a, x, 0:BLOCK] = zero

    def fill_coef(lo, hi):
        @pl.loop(0, (hi - lo) // BLOCK)
        def _(i):
            here = pl.ds(pl.multiple_of(lo + i * BLOCK, BLOCK), BLOCK)
            for x in range(planes):
                label = lab[x, here]
                masks = [label == k for k in range(table.shape[1])]
                for which in range(4):
                    picked = zero
                    for k, mask in enumerate(masks):
                        picked = picked + jnp.where(mask, table[which, k], jnp.float32(0.0))
                    coef[which, x, here] = picked

    def turn_rows(ref, lo, hi, turn):
        @pl.loop(0, (hi - lo) // BLOCK)
        def _(i):
            here = pl.ds(pl.multiple_of(lo + i * BLOCK, BLOCK), BLOCK)
            for x in range(planes):
                for a in range(3):
                    re_new, im_new = turned(ref[0, a, x, here], ref[1, a, x, here], *turn)
                    ref[0, a, x, here] = re_new
                    ref[1, a, x, here] = im_new

    def prepare(c, t):
        stage_e, stage_h = stages[c][:2]
        last = planes - 1

        def one(i, carry):
            at = BASE + starts[c] - t + i * BLOCK
            here, up = pl.ds(at, BLOCK), pl.ds(at + 1, BLOCK)
            to = pl.ds(pl.multiple_of(i * BLOCK, BLOCK), BLOCK)
            for ri in range(2):
                stage_e[ri, 0, to] = e[ri, 1, 0, here]
                stage_e[ri, 1, to] = e[ri, 2, 0, here]
                ex, ey, ez = [e[ri, a, last, here] for a in range(3)]
                hy = h[ri, 1, last, here] - time_step * ((next_z(ex) - ex) + ez)
                hz = h[ri, 2, last, here] + time_step * (ey + (e[ri, 0, last, up] - ex))
                h[ri, 1, last, here] = hy
                h[ri, 2, last, here] = hz
                stage_h[ri, 0, to] = hy
                stage_h[ri, 1, to] = hz
            return carry
        lax.fori_loop(0, sizes[c] // BLOCK, one, 0, unroll=UNROLL)
        par = lax.rem(t, 2)
        send_h(c, par).start()
        send_e(c, par).start()

    def advance(c, t):
        par = lax.rem(t, 2)
        send_h(c, par).wait_recv()
        send_e(c, par).wait_recv()
        ge, gh = stages[c][2].at[par], stages[c][3].at[par]

        def one(i, carry):
            at = BASE + starts[c] - t + i * BLOCK
            here, up, down = pl.ds(at, BLOCK), pl.ds(at + 1, BLOCK), pl.ds(at - 1, BLOCK)
            to = pl.ds(pl.multiple_of(i * BLOCK, BLOCK), BLOCK)
            field = [[e[ri, a, 0, here] for a in range(3)] for ri in range(2)]
            before = [turned(gh[0, a, to], gh[1, a, to], *turn_l) for a in range(2)]
            prev_y = [before[0][ri] + time_step * field[ri][2] for ri in range(2)]
            prev_zz = [before[1][ri] - time_step * field[ri][1] for ri in range(2)]
            for x in range(planes):
                at_last = x == planes - 1
                if at_last:
                    beyond = [turned(ge[0, a, to], ge[1, a, to], *turn_r) for a in range(2)]
                else:
                    later = [[e[ri, a, x + 1, here] for a in range(3)] for ri in range(2)]
                new = []
                for ri in range(2):
                    ex, ey, ez = field[ri]
                    hx = h[ri, 0, x, here] - time_step * ((e[ri, 2, x, up] - ez) - (next_z(ey) - ey))
                    if at_last:
                        hy = h[ri, 1, x, here] + time_step * beyond[1][ri]
                        hz = h[ri, 2, x, here] - time_step * beyond[0][ri]
                    else:
                        hy = h[ri, 1, x, here] - time_step * ((next_z(ex) - ex) - (later[ri][2] - ez))
                        hz = h[ri, 2, x, here] - time_step * ((later[ri][1] - ey) - (e[ri, 0, x, up] - ex))
                    h[ri, 0, x, here] = hx
                    h[ri, 1, x, here] = hy
                    h[ri, 2, x, here] = hz
                    new.append((hx, hy, hz))
                ce, ja, jb, de = [coef[k, x, here] for k in range(4)]
                for ri in range(2):
                    hx, hy, hz = new[ri]
                    kx = (hz - h[ri, 2, x, down]) - (hy - prev_z(hy))
                    ky = (hx - prev_z(hx)) - (hz - prev_zz[ri])
                    kz = (hy - prev_y[ri]) - (hx - h[ri, 0, x, down])
                    for a, kurl in enumerate((kx, ky, kz)):
                        polar = pol[ri, a, x, here]
                        current = ja * cur[ri, a, x, here] + jb * (de * field[ri][a] - polar)
                        cur[ri, a, x, here] = current
                        pol[ri, a, x, here] = polar + time_step * current
                        e[ri, a, x, here] = field[ri][a] + ce * (kurl - current)
                    prev_y[ri], prev_zz[ri] = hy, hz
                if not at_last:
                    field = later
            return carry
        lax.fori_loop(0, sizes[c] // BLOCK, one, 0, unroll=1)

    def arrive(c):
        mine = [n for n, (chunk, _) in enumerate(segments) if chunk == c]
        for n in mine:
            wait_in(n, 0)
        for n in mine:
            lo, hi = segments[n][1]
            fill_coef(lo, hi)
        for n in mine:
            lo, hi = segments[n][1]
            for k, ref in ((1, e), (2, h)):
                wait_in(n, k)
                if hi <= LOW:
                    turn_rows(ref, lo, hi, turn_low)
                if lo >= LOW + half:
                    turn_rows(ref, lo, hi, turn_high)
        prepare(c, 1)

    waves = LAG * (CHUNKS - 1) + ITERS + 1

    @pl.loop(0, waves)
    def _(w):
        for c in range(CHUNKS):
            t = w - LAG * c

            @pl.when((t >= 1) & (t <= ITERS))
            def _():
                advance(c, t)
                send_h(c, 0).wait_send()
                send_e(c, 0).wait_send()

                @pl.when(t < ITERS)
                def _():
                    prepare(c, t + 1)

                @pl.when(t == ITERS)
                def _():
                    each_move_out(c, start)

        for c in range(CHUNKS):
            @pl.when(w == LAG * c)
            def _():
                arrive(c)

    for n in range(len(segments)):
        each_move_in(n, sent)
    for c in range(CHUNKS):
        each_move_out(c, sent)
        wait_out(c)


def shards(e_field, h_field, labels, kpoint, eps_inf, delta_eps, omega_zero, damping):
    theta_x = jnp.float32(2.0 * math.pi) * kpoint[0].astype(jnp.float32) / KGRID
    theta_y = jnp.float32(2.0 * math.pi) * kpoint[1].astype(jnp.float32) / KGRID
    cos_x, sin_x = (jnp.cos(theta_x), jnp.sin(theta_x))
    cos_y, sin_y = (jnp.cos(theta_y), jnp.sin(theta_y))
    damped = damping * time_step / 2.0
    table = jnp.stack([
        time_step / eps_inf,
        (1.0 - damped) / (1.0 + damped),
        time_step * omega_zero * omega_zero / (1.0 + damped),
        delta_eps,
    ])
    position = lax.axis_index("gx")
    size = lax.axis_size("gx")
    one, nought = jnp.float32(1.0), jnp.float32(0.0)
    y = lax.rem(lax.div(position, 2), 2)
    first = (position < 4) & (lax.rem(position, 2) == 0)
    last = (position >= size - 4) & (lax.rem(position, 2) == 1)

    def turn(where, cosv, sinv):
        return [jnp.where(where, cosv, one), jnp.where(where, sinv, nought)]

    phase = jnp.stack(
        turn(last, cos_x, sin_x) + turn(first, cos_x, -sin_x)
        + turn(y == 0, cos_y, -sin_y) + turn(y == 1, cos_y, sin_y))
    local, total_rows, width = labels.shape
    half = total_rows // 2
    planes = 2 * local
    rows = half + LOW + GHOST
    state = (2, 3, local, total_rows, width)
    field = (2, 3, planes, rows, width)
    count = sum(len(p) for p in pieces_in(half))
    dma = pltpu.SemaphoreType.DMA
    anywhere = pl.BlockSpec(memory_space=pl.ANY)
    scalars = pl.BlockSpec(memory_space=pltpu.SMEM)
    halos = []
    for size in chunk_sizes(half):
        halos += [pltpu.VMEM((2, 2, size, width), jnp.float32)] * 2
        halos += [pltpu.VMEM((2, 2, 2, size, width), jnp.float32)] * 2
    return pl.pallas_call(
        kernel,
        out_shape=(jax.ShapeDtypeStruct(state, jnp.float32),) * 2,
        in_specs=[anywhere] * 3 + [scalars] * 2,
        out_specs=(anywhere, anywhere),
        scratch_shapes=[pltpu.VMEM(field, jnp.float32)] * 4
        + [pltpu.VMEM((4, planes, rows, width), jnp.float32), pltpu.VMEM((planes, rows, width), jnp.int32)]
        + halos
        + [dma((count, 3, 2)), dma((count, 3, 2)), dma((CHUNKS,)), dma((CHUNKS, 2)),
           dma((CHUNKS,)), dma((CHUNKS, 2)), dma((CHUNKS, 2, 2)), dma((CHUNKS, 2, 2))],
        compiler_params=pltpu.CompilerParams(collective_id=0, has_side_effects=True),
    )(e_field, h_field, labels, table, phase)


def solution(mesh):
    placed = (
        P(None, None, ("kpt", "gx"), None, None),
        P(None, None, ("kpt", "gx"), None, None),
        P(("kpt", "gx"), None, None),
        P("kpt"),
        P(),
        P(),
        P(),
        P(),
    )
    return jax.shard_map(
        shards,
        mesh=mesh,
        in_specs=placed,
        out_specs=(
            P(None, None, ("kpt", "gx"), None, None),
            P(None, None, ("kpt", "gx"), None, None),
        ),
        check_vma=False,
    )
```

time: 244 us -> 219 us (0.90)
  Pallas kernels: 232 us -> 207 us
    pallas_call x1, Pallas kernels: 232 us -> 207 us  [shards(): pl.pallas_call(kernel, out_shape=(jax.ShapeDtypeStruct(state, jnp.float32...]
where the time goes in v1:
time: 219 us; the launch traced here: 218 us
  Pallas kernels  207 us (95%)
  local copies, waits for them, and re-layouts  7.49 us (3%)
  between operations  2.31 us (1%)
    pallas_call x1, Pallas kernels, shards(): pl.pallas_call(kernel, out_shape=(jax.ShapeDtypeStruct(state, jnp.float32...  207 us
    unnamed x4, local copies, waits for them, and re-layouts  5.57 us

profile of v1, /device:TPU:1, one launch (start us, length us, event | category | flops | bytes accessed | tf_op | source)
XLA Modules:
  0.0 218.5 jit_solution(7008999307123840161)
XLA Ops:
  0.7 1.3 fusion.3
  3.6 0.6 stack.55.phase
  4.2 0.7 fusion.1
  4.9 1.2 pad_maximum_fusion.table
  6.1 206.7 %shard_map.95 = (f32[2,3,2,512,128]{4,3,2,1,0:T(8,128)}, f32[2,3,2,512,128]{4,3,2,1,0:T(8,128)}) custom-call(f32[2,3,2,512,128]{4,3,2,1,0:T(8,128)} %e_in.1, f32[2,3,2,512,128]{4,3,2,1,0:T(8,128)} %h_in.1, s32[2,512,128]{2,1,0:T(8,128)} %lab_in.1, f32[4,4]{1,0:T(4,128)} %pad_maximum_fusion.table, f32[8]{0:T(128)} %stack.55.phase), custom_call_target="tpu_custom_call" | custom-call | tf_op jit(solution)/shard_map/pallas_call | solution.py:380
  212.9 0.0 copy-start
  212.9 3.9 %copy.12 = f32[2,3,2,512,128]{4,3,2,1,0:T(8,128)} copy(f32[2,3,2,512,128]{4,3,2,1,0:T(8,128)} %get-tuple-element.9) | data formatting | bytes 6291456
  216.8 0.0 copy-done
  216.8 1.7 copy.13
Async XLA Ops:
  212.9 3.9 %copy-start = (f32[2,3,2,512,128]{4,3,2,1,0:T(8,128)S(1)}, f32[2,3,2,512,128]{4,3,2,1,0:T(8,128)}, u32[]{:S(2)}) copy-start(f32[2,3,2,512,128]{4,3,2,1,0:T(8,128)} %get-tuple-element.10) | copy-start | bytes 9437188

commit v2 on v1

--- a/solution.py
+++ b/solution.py
@@ -10,9 +10,12 @@
 ITERS = 12
 KGRID = 16
 BLOCK = 8
-CHUNKS = 7
-LAG = 2
-UNROLL = 5
+SHARES = (3, 3, 3, 3, 3, 3, 3, 3, 3, 3, 3, 2)
+BEGIN = (0, 1, 3, 4, 6, 7, 9, 10, 12, 13, 15, 16)
+CHUNKS = len(SHARES)
+UNROLL_P = 3
+UNROLL_H = 3
+UNROLL_E = 3
 LOW = 24
 GHOST = 16
 BASE = 13
@@ -26,7 +29,8 @@
 
 def chunk_sizes(half):
     blocks = (half + 24) // BLOCK
-    return [BLOCK * (blocks // CHUNKS + (c < blocks % CHUNKS)) for c in range(CHUNKS)]
+    ends = [blocks * sum(SHARES[:c]) // sum(SHARES) for c in range(CHUNKS + 1)]
+    return [BLOCK * (ends[c + 1] - ends[c]) for c in range(CHUNKS)]
 
 
 def edges_of(half):
@@ -52,8 +56,8 @@
     return [(max(starts[c], LOW), min(starts[c + 1], LOW + half)) for c in range(CHUNKS)]
 
 
-def kernel(e_in, h_in, lab_in, table, phase, e_out, h_out,
-           e, h, pol, cur, coef, lab, *scratch):
+def kernel(e_in, h_in, lab_in, kpoint, eps_inf, delta_eps, omega_zero, damping, e_out, h_out,
+           e, h, pol, cur, coef, lab, table, phase, *scratch):
     stages = [scratch[4 * c:4 * c + 4] for c in range(CHUNKS)]
     in_send, in_recv, se, re, sh, rh, so, ro = scratch[4 * CHUNKS:]
     gx = lax.axis_size("gx")
@@ -71,8 +75,10 @@
     starts = edges_of(half)
     sizes = chunk_sizes(half)
     ins, outs = pieces_in(half), pieces_out(half)
-    ph = [phase[i] for i in range(8)]
-    turn_r, turn_l, turn_low, turn_high = [(ph[2 * i], ph[2 * i + 1]) for i in range(4)]
+    labels = eps_inf.shape[0]
+
+    def turn_of(i):
+        return phase[2 * i], phase[2 * i + 1]
 
     def remote(src, dst, send, recv, to):
         return pltpu.make_async_remote_copy(
@@ -123,6 +129,28 @@
     for n in range(len(segments)):
         each_move_in(n, start)
 
+    def spread(value):
+        return jnp.full((BLOCK, width), value, jnp.float32)
+
+    for k in range(labels):
+        damped = spread(damping[k]) * time_step / 2.0
+        omega = spread(omega_zero[k])
+        table[k] = time_step / spread(eps_inf[k])
+        table[labels + k] = (1.0 - damped) / (1.0 + damped)
+        table[2 * labels + k] = time_step * omega * omega / (1.0 + damped)
+        table[3 * labels + k] = spread(delta_eps[k])
+
+    cos_sin = []
+    for axis in range(2):
+        theta = spread(2.0 * math.pi) * spread(kpoint[axis].astype(jnp.float32)) / KGRID
+        cos_sin.append((jnp.cos(theta), jnp.sin(theta)))
+    (cos_x, sin_x), (cos_y, sin_y) = cos_sin
+    turns = (((me >= gx - 4) & (core == 1), cos_x, sin_x), ((me < 4) & (core == 0), cos_x, -sin_x),
+             (y == 0, cos_y, -sin_y), (y == 1, cos_y, sin_y))
+    for i, (where, cosv, sinv) in enumerate(turns):
+        phase[2 * i] = jnp.where(where, cosv, 1.0)
+        phase[2 * i + 1] = jnp.where(where, sinv, 0.0)
+
     def wait_in(n, k):
         for slot in range(2):
             src, dst = move_in(n, 0, slot)[k]
@@ -155,16 +183,42 @@
                 src, dst = move_out(c, k, 0)
                 remote(src, dst, so.at[c, k, 0], ro.at[c, k, other], base + lax.rem(q + 1, 4)).wait_recv()
 
-    def send_e(c, par):
-        return remote(stages[c][0], stages[c][2].at[par], se.at[c], re.at[c, par], left)
-
-    def send_h(c, par):
-        return remote(stages[c][1], stages[c][3].at[par], sh.at[c], rh.at[c, par], right)
+    def halos(c, t, act):
+        par = lax.rem(t, 2)
+
+        def both(cut):
+            kept = pl.ds(cut, sizes[c] - cut)
+            for k, (send, recv, to) in enumerate(((se, re, left), (sh, rh, right))):
+                act(remote(stages[c][k].at[:, :, kept], stages[c][2 + k].at[par, :, :, kept],
+                           send.at[c], recv.at[c, par], to))
+
+        if c:
+            both(0)
+        else:
+            for k in range((ITERS - 1) // 4 + 1):
+                @pl.when(lax.div(t - 1, 4) == k)
+                def _():
+                    both(BLOCK * k)
+
+    def block_loop(c, t, body, unroll):
+        count = sizes[c] // BLOCK
+        first = 0
+        if not c:
+            first = (ITERS - 1) // 4
+            for i in range(first):
+                @pl.when(lax.div(t - 1, 4) <= i)
+                def _():
+                    body(i, 0)
+        left_over = count - first
+        lax.fori_loop(first, count, body, 0, unroll=unroll if left_over % unroll == 0 else 1)
 
     lane = lax.broadcasted_iota(jnp.int32, (BLOCK, width), 1)
     not_end = lane < width - 1
     not_start = lane > 0
     zero = jnp.zeros((BLOCK, width), jnp.float32)
+
+    def rows_at(i):
+        return pl.ds(i * BLOCK if isinstance(i, int) else pl.multiple_of(i * BLOCK, BLOCK), BLOCK)
 
     def next_z(f):
         return jnp.where(not_end, pltpu.roll(f, width - 1, 1), 0.0)
@@ -195,11 +249,11 @@
             here = pl.ds(pl.multiple_of(lo + i * BLOCK, BLOCK), BLOCK)
             for x in range(planes):
                 label = lab[x, here]
-                masks = [label == k for k in range(table.shape[1])]
+                masks = [label == k for k in range(labels)]
                 for which in range(4):
                     picked = zero
                     for k, mask in enumerate(masks):
-                        picked = picked + jnp.where(mask, table[which, k], jnp.float32(0.0))
+                        picked = picked + jnp.where(mask, table[which * labels + k], 0.0)
                     coef[which, x, here] = picked
 
     def turn_rows(ref, lo, hi, turn):
@@ -212,14 +266,17 @@
                     ref[0, a, x, here] = re_new
                     ref[1, a, x, here] = im_new
 
+    last = planes - 1
+
+    def spots(c, t, i):
+        at = BASE + starts[c] - t + i * BLOCK
+        return [pl.ds(at + k, BLOCK) for k in (-1, 0, 1)] + [rows_at(i)]
+
     def prepare(c, t):
         stage_e, stage_h = stages[c][:2]
-        last = planes - 1
 
         def one(i, carry):
-            at = BASE + starts[c] - t + i * BLOCK
-            here, up = pl.ds(at, BLOCK), pl.ds(at + 1, BLOCK)
-            to = pl.ds(pl.multiple_of(i * BLOCK, BLOCK), BLOCK)
+            down, here, up, to = spots(c, t, i)
             for ri in range(2):
                 stage_e[ri, 0, to] = e[ri, 1, 0, here]
                 stage_e[ri, 1, to] = e[ri, 2, 0, here]
@@ -231,62 +288,83 @@
                 stage_h[ri, 0, to] = hy
                 stage_h[ri, 1, to] = hz
             return carry
-        lax.fori_loop(0, sizes[c] // BLOCK, one, 0, unroll=UNROLL)
-        par = lax.rem(t, 2)
-        send_h(c, par).start()
-        send_e(c, par).start()
-
-    def advance(c, t):
-        par = lax.rem(t, 2)
-        send_h(c, par).wait_recv()
-        send_e(c, par).wait_recv()
-        ge, gh = stages[c][2].at[par], stages[c][3].at[par]
-
+        block_loop(c, t, one, UNROLL_P)
+        halos(c, t, lambda copy: copy.start())
+
+    def inner(c, t):
         def one(i, carry):
-            at = BASE + starts[c] - t + i * BLOCK
-            here, up, down = pl.ds(at, BLOCK), pl.ds(at + 1, BLOCK), pl.ds(at - 1, BLOCK)
-            to = pl.ds(pl.multiple_of(i * BLOCK, BLOCK), BLOCK)
+            down, here, up, to = spots(c, t, i)
             field = [[e[ri, a, 0, here] for a in range(3)] for ri in range(2)]
-            before = [turned(gh[0, a, to], gh[1, a, to], *turn_l) for a in range(2)]
-            prev_y = [before[0][ri] + time_step * field[ri][2] for ri in range(2)]
-            prev_zz = [before[1][ri] - time_step * field[ri][1] for ri in range(2)]
             for x in range(planes):
-                at_last = x == planes - 1
-                if at_last:
-                    beyond = [turned(ge[0, a, to], ge[1, a, to], *turn_r) for a in range(2)]
-                else:
+                if x < last:
                     later = [[e[ri, a, x + 1, here] for a in range(3)] for ri in range(2)]
-                new = []
                 for ri in range(2):
                     ex, ey, ez = field[ri]
-                    hx = h[ri, 0, x, here] - time_step * ((e[ri, 2, x, up] - ez) - (next_z(ey) - ey))
-                    if at_last:
-                        hy = h[ri, 1, x, here] + time_step * beyond[1][ri]
-                        hz = h[ri, 2, x, here] - time_step * beyond[0][ri]
-                    else:
-                        hy = h[ri, 1, x, here] - time_step * ((next_z(ex) - ex) - (later[ri][2] - ez))
-                        hz = h[ri, 2, x, here] - time_step * ((later[ri][1] - ey) - (e[ri, 0, x, up] - ex))
-                    h[ri, 0, x, here] = hx
-                    h[ri, 1, x, here] = hy
-                    h[ri, 2, x, here] = hz
-                    new.append((hx, hy, hz))
+                    h[ri, 0, x, here] = h[ri, 0, x, here] - time_step * ((e[ri, 2, x, up] - ez) - (next_z(ey) - ey))
+                    if x < last:
+                        h[ri, 1, x, here] = h[ri, 1, x, here] - time_step * ((next_z(ex) - ex) - (later[ri][2] - ez))
+                        h[ri, 2, x, here] = h[ri, 2, x, here] - time_step * ((later[ri][1] - ey) - (e[ri, 0, x, up] - ex))
+                field = later
+            return carry
+        block_loop(c, t, one, UNROLL_H)
+
+    def complete(c, t):
+        ge = stages[c][2].at[lax.rem(t, 2)]
+
+        def one(i, carry):
+            down, here, up, to = spots(c, t, i)
+            beyond = [turned(ge[0, a, to], ge[1, a, to], *turn_of(0)) for a in range(2)]
+            for ri in range(2):
+                h[ri, 1, last, here] = h[ri, 1, last, here] + time_step * beyond[1][ri]
+                h[ri, 2, last, here] = h[ri, 2, last, here] - time_step * beyond[0][ri]
+            return carry
+        block_loop(c, t, one, UNROLL_P)
+
+    def electric(c, t, order):
+        gh = stages[c][3].at[lax.rem(t, 2)]
+
+        def one(i, carry):
+            down, here, up, to = spots(c, t, i)
+            for x in order:
+                if x:
+                    prev_y, prev_zz = [[h[ri, a, x - 1, here] for ri in range(2)] for a in (1, 2)]
+                else:
+                    before = [turned(gh[0, a, to], gh[1, a, to], *turn_of(1)) for a in range(2)]
+                    prev_y = [before[0][ri] + time_step * e[ri, 2, 0, here] for ri in range(2)]
+                    prev_zz = [before[1][ri] - time_step * e[ri, 1, 0, here] for ri in range(2)]
                 ce, ja, jb, de = [coef[k, x, here] for k in range(4)]
                 for ri in range(2):
-                    hx, hy, hz = new[ri]
+                    hx, hy, hz = [h[ri, a, x, here] for a in range(3)]
                     kx = (hz - h[ri, 2, x, down]) - (hy - prev_z(hy))
                     ky = (hx - prev_z(hx)) - (hz - prev_zz[ri])
                     kz = (hy - prev_y[ri]) - (hx - h[ri, 0, x, down])
                     for a, kurl in enumerate((kx, ky, kz)):
-                        polar = pol[ri, a, x, here]
-                        current = ja * cur[ri, a, x, here] + jb * (de * field[ri][a] - polar)
+                        field, polar = e[ri, a, x, here], pol[ri, a, x, here]
+                        current = ja * cur[ri, a, x, here] + jb * (de * field - polar)
                         cur[ri, a, x, here] = current
                         pol[ri, a, x, here] = polar + time_step * current
-                        e[ri, a, x, here] = field[ri][a] + ce * (kurl - current)
-                    prev_y[ri], prev_zz[ri] = hy, hz
-                if not at_last:
-                    field = later
+                        e[ri, a, x, here] = field + ce * (kurl - current)
             return carry
-        lax.fori_loop(0, sizes[c] // BLOCK, one, 0, unroll=1)
+        block_loop(c, t, one, UNROLL_E)
+
+    def advance(c, t):
+        halos(c, t, lambda copy: copy.wait_recv())
+        complete(c, t)
+        electric(c, t, (0, last))
+        halos(c, t, lambda copy: copy.wait_send())
+
+        @pl.when(t < ITERS)
+        def _():
+            prepare(c, t + 1)
+        electric(c, t, range(1, last))
+
+        @pl.when(t < ITERS)
+        def _():
+            inner(c, t + 1)
+
+        @pl.when(t == ITERS)
+        def _():
+            each_move_out(c, start)
 
     def arrive(c):
         mine = [n for n, (chunk, _) in enumerate(segments) if chunk == c]
@@ -300,34 +378,25 @@
             for k, ref in ((1, e), (2, h)):
                 wait_in(n, k)
                 if hi <= LOW:
-                    turn_rows(ref, lo, hi, turn_low)
+                    turn_rows(ref, lo, hi, turn_of(2))
                 if lo >= LOW + half:
-                    turn_rows(ref, lo, hi, turn_high)
+                    turn_rows(ref, lo, hi, turn_of(3))
         prepare(c, 1)
-
-    waves = LAG * (CHUNKS - 1) + ITERS + 1
+        inner(c, 1)
+
+    waves = BEGIN[-1] + ITERS + 1
 
     @pl.loop(0, waves)
     def _(w):
         for c in range(CHUNKS):
-            t = w - LAG * c
+            t = w - BEGIN[c]
 
             @pl.when((t >= 1) & (t <= ITERS))
             def _():
                 advance(c, t)
-                send_h(c, 0).wait_send()
-                send_e(c, 0).wait_send()
-
-                @pl.when(t < ITERS)
-                def _():
-                    prepare(c, t + 1)
-
-                @pl.when(t == ITERS)
-                def _():
-                    each_move_out(c, start)
 
         for c in range(CHUNKS):
-            @pl.when(w == LAG * c)
+            @pl.when(w == BEGIN[c])
             def _():
                 arrive(c)
 
@@ -339,30 +408,6 @@
 
 
 def shards(e_field, h_field, labels, kpoint, eps_inf, delta_eps, omega_zero, damping):
-    theta_x = jnp.float32(2.0 * math.pi) * kpoint[0].astype(jnp.float32) / KGRID
-    theta_y = jnp.float32(2.0 * math.pi) * kpoint[1].astype(jnp.float32) / KGRID
-    cos_x, sin_x = (jnp.cos(theta_x), jnp.sin(theta_x))
-    cos_y, sin_y = (jnp.cos(theta_y), jnp.sin(theta_y))
-    damped = damping * time_step / 2.0
-    table = jnp.stack([
-        time_step / eps_inf,
-        (1.0 - damped) / (1.0 + damped),
-        time_step * omega_zero * omega_zero / (1.0 + damped),
-        delta_eps,
-    ])
-    position = lax.axis_index("gx")
-    size = lax.axis_size("gx")
-    one, nought = jnp.float32(1.0), jnp.float32(0.0)
-    y = lax.rem(lax.div(position, 2), 2)
-    first = (position < 4) & (lax.rem(position, 2) == 0)
-    last = (position >= size - 4) & (lax.rem(position, 2) == 1)
-
-    def turn(where, cosv, sinv):
-        return [jnp.where(where, cosv, one), jnp.where(where, sinv, nought)]
-
-    phase = jnp.stack(
-        turn(last, cos_x, sin_x) + turn(first, cos_x, -sin_x)
-        + turn(y == 0, cos_y, -sin_y) + turn(y == 1, cos_y, sin_y))
     local, total_rows, width = labels.shape
     half = total_rows // 2
     planes = 2 * local
@@ -380,15 +425,16 @@
     return pl.pallas_call(
         kernel,
         out_shape=(jax.ShapeDtypeStruct(state, jnp.float32),) * 2,
-        in_specs=[anywhere] * 3 + [scalars] * 2,
+        in_specs=[anywhere] * 3 + [scalars] * 5,
         out_specs=(anywhere, anywhere),
         scratch_shapes=[pltpu.VMEM(field, jnp.float32)] * 4
-        + [pltpu.VMEM((4, planes, rows, width), jnp.float32), pltpu.VMEM((planes, rows, width), jnp.int32)]
+        + [pltpu.VMEM((4, planes, rows, width), jnp.float32), pltpu.VMEM((planes, rows, width), jnp.int32),
+           pltpu.VMEM((4 * eps_inf.shape[0], BLOCK, width), jnp.float32), pltpu.VMEM((8, BLOCK, width), jnp.float32)]
         + halos
         + [dma((count, 3, 2)), dma((count, 3, 2)), dma((CHUNKS,)), dma((CHUNKS, 2)),
            dma((CHUNKS,)), dma((CHUNKS, 2)), dma((CHUNKS, 2, 2)), dma((CHUNKS, 2, 2))],
         compiler_params=pltpu.CompilerParams(collective_id=0, has_side_effects=True),
-    )(e_field, h_field, labels, table, phase)
+    )(e_field, h_field, labels, kpoint, eps_inf, delta_eps, omega_zero, damping)
 
 
 def solution(mesh):

time: 219 us -> 201 us (0.918)
  Pallas kernels: 207 us -> 194 us
    pallas_call x1, Pallas kernels: 207 us -> 194 us  [shards(): pl.pallas_call(kernel, out_shape=(jax.ShapeDtypeStruct(state, jnp.float32...]
where the time goes in v2:
time: 201 us; the launch traced here: 200 us
  Pallas kernels  194 us (97%)
  local copies, waits for them, and re-layouts  5.57 us (3%)
    pallas_call x1, Pallas kernels, shards(): pl.pallas_call(kernel, out_shape=(jax.ShapeDtypeStruct(state, jnp.float32...  194 us
    unnamed x4, local copies, waits for them, and re-layouts  5.57 us

profile of v2, /device:TPU:1, one launch (start us, length us, event | category | flops | bytes accessed | tf_op | source)
XLA Modules:
  0.0 200.4 jit_solution(12188516958105165903)
XLA Ops:
  0.6 194.2 %shard_map.95 = (f32[2,3,2,512,128]{4,3,2,1,0:T(8,128)}, f32[2,3,2,512,128]{4,3,2,1,0:T(8,128)}) custom-call(f32[2,3,2,512,128]{4,3,2,1,0:T(8,128)} %e_in.1, f32[2,3,2,512,128]{4,3,2,1,0:T(8,128)} %h_in.1, s32[2,512,128]{2,1,0:T(8,128)} %lab_in.1, s32[2]{0:T(128)} %kpoint.1, f32[4]{0:T(128)} %eps_inf.1, f32[4]{0:T(128)} %delta_eps.1, f32[4]{0:T(128)} %omega_zero.1, ...), custom_call_target="tpu_custom_call" | custom-call | tf_op jit(solution)/shard_map/pallas_call | solution.py:425
  194.8 0.0 copy-start
  194.8 3.9 %copy.12 = f32[2,3,2,512,128]{4,3,2,1,0:T(8,128)} copy(f32[2,3,2,512,128]{4,3,2,1,0:T(8,128)} %get-tuple-element.4) | data formatting | bytes 6291456
  198.7 0.0 copy-done
  198.7 1.7 copy.13
Async XLA Ops:
  194.8 3.9 %copy-start = (f32[2,3,2,512,128]{4,3,2,1,0:T(8,128)S(1)}, f32[2,3,2,512,128]{4,3,2,1,0:T(8,128)}, u32[]{:S(2)}) copy-start(f32[2,3,2,512,128]{4,3,2,1,0:T(8,128)} %get-tuple-element.5) | copy-start | bytes 9437188

commit v3 on v2

--- a/solution.py
+++ b/solution.py
@@ -10,12 +10,12 @@
 ITERS = 12
 KGRID = 16
 BLOCK = 8
-SHARES = (3, 3, 3, 3, 3, 3, 3, 3, 3, 3, 3, 2)
-BEGIN = (0, 1, 3, 4, 6, 7, 9, 10, 12, 13, 15, 16)
+SHARES = (3, 2, 2, 2, 2, 2, 2, 2, 2, 2, 2, 2, 2, 2, 2, 2, 2)
+BEGIN = (0, 1, 2, 3, 4, 5, 6, 7, 8, 9, 10, 11, 12, 13, 14, 15, 16)
 CHUNKS = len(SHARES)
-UNROLL_P = 3
-UNROLL_H = 3
-UNROLL_E = 3
+UNROLL_P = 2
+UNROLL_H = 2
+UNROLL_E = 2
 LOW = 24
 GHOST = 16
 BASE = 13
@@ -100,9 +100,9 @@
         first = (dest * half + lo - LOW) % total_rows
         src, dst = pl.ds(first, hi - lo), pl.ds(lo, hi - lo)
         group = pl.ds(slot * local, local)
-        return ((lab_in.at[:, src], lab.at[group, dst]),
-                (e_in.at[:, :, :, src], e.at[:, :, group, dst]),
-                (h_in.at[:, :, :, src], h.at[:, :, group, dst]))
+        return ((e_in.at[:, :, :, src], e.at[:, :, group, dst]),
+                (h_in.at[:, :, :, src], h.at[:, :, group, dst]),
+                (lab_in.at[:, src], lab.at[group, dst]))
 
     def each_move_in(n, act):
         for dest in range(2):
@@ -369,13 +369,8 @@
     def arrive(c):
         mine = [n for n, (chunk, _) in enumerate(segments) if chunk == c]
         for n in mine:
-            wait_in(n, 0)
-        for n in mine:
             lo, hi = segments[n][1]
-            fill_coef(lo, hi)
-        for n in mine:
-            lo, hi = segments[n][1]
-            for k, ref in ((1, e), (2, h)):
+            for k, ref in enumerate((e, h)):
                 wait_in(n, k)
                 if hi <= LOW:
                     turn_rows(ref, lo, hi, turn_of(2))
@@ -383,6 +378,9 @@
                     turn_rows(ref, lo, hi, turn_of(3))
         prepare(c, 1)
         inner(c, 1)
+        for n in mine:
+            wait_in(n, 2)
+            fill_coef(*segments[n][1])
 
     waves = BEGIN[-1] + ITERS + 1
 

time: 201 us -> 197 us (0.980)
  Pallas kernels: 194 us -> 191 us
    pallas_call x1, Pallas kernels: 194 us -> 191 us  [shards(): pl.pallas_call(kernel, out_shape=(jax.ShapeDtypeStruct(state, jnp.float32...]
where the time goes in v3:
time: 197 us
  Pallas kernels  191 us (97%)
  local copies, waits for them, and re-layouts  5.57 us (3%)
    pallas_call x1, Pallas kernels, shards(): pl.pallas_call(kernel, out_shape=(jax.ShapeDtypeStruct(state, jnp.float32...  191 us
    unnamed x4, local copies, waits for them, and re-layouts  5.57 us

profile of v3, /device:TPU:1, one launch (start us, length us, event | category | flops | bytes accessed | tf_op | source)
XLA Modules:
  0.0 197.0 jit_solution(9087816140836995550)
XLA Ops:
  0.6 190.8 %shard_map.95 = (f32[2,3,2,512,128]{4,3,2,1,0:T(8,128)}, f32[2,3,2,512,128]{4,3,2,1,0:T(8,128)}) custom-call(f32[2,3,2,512,128]{4,3,2,1,0:T(8,128)} %e_in.1, f32[2,3,2,512,128]{4,3,2,1,0:T(8,128)} %h_in.1, s32[2,512,128]{2,1,0:T(8,128)} %lab_in.1, s32[2]{0:T(128)} %kpoint.1, f32[4]{0:T(128)} %eps_inf.1, f32[4]{0:T(128)} %delta_eps.1, f32[4]{0:T(128)} %omega_zero.1, ...), custom_call_target="tpu_custom_call" | custom-call | tf_op jit(solution)/shard_map/pallas_call | solution.py:423
  191.4 0.0 copy-start
  191.5 3.9 %copy.12 = f32[2,3,2,512,128]{4,3,2,1,0:T(8,128)} copy(f32[2,3,2,512,128]{4,3,2,1,0:T(8,128)} %get-tuple-element.4) | data formatting | bytes 6291456
  195.4 0.0 copy-done
  195.4 1.7 copy.13
Async XLA Ops:
  191.4 3.9 %copy-start = (f32[2,3,2,512,128]{4,3,2,1,0:T(8,128)S(1)}, f32[2,3,2,512,128]{4,3,2,1,0:T(8,128)}, u32[]{:S(2)}) copy-start(f32[2,3,2,512,128]{4,3,2,1,0:T(8,128)} %get-tuple-element.5) | copy-start | bytes 9437188
